TPU v7x, 16 devices: a whole 2x2x2 slice. The times are simulated.
16 devices in a mesh: tp: 2 (over z), y: 2 (over y), x: 4 (over x, core).
Axes of the slice: x: 2, y: 2, z: 2, core: 2. Of those that a mesh axis runs over, the one named last changes fastest.
Arguments:
- w_up: float32 [4, 2, 1, 1280, 5120], P('x', 'y', None, None, 'tp')
- w_down: float32 [4, 2, 1, 5120, 1280], P('x', 'y', None, 'tp')
- inputs: bfloat16 [4, 2, 3, 4096, 1280], P('x', 'y')
- targets: bfloat16 [4, 2, 3, 4096, 1280], P('x', 'y')
Outputs:
- output 1: float32 [4, 2, 1, 1280, 5120], P('x', 'y', None, None, 'tp')
- output 2: float32 [4, 2, 1, 5120, 1280], P('x', 'y', None, 'tp')
- output 3: bfloat16 [4, 2, 4096, 1280], P('x', 'y')
All inputs are finite; a program needn't handle non-finite values.
Results may differ from a plain program's by a relative error of at most 0.00216668.
Values are sent between devices in bfloat16 or wider.
A program may use at most 1 GiB of HBM per device.

v0:
```python
import jax
import jax.numpy as jnp
from jax import lax
from jax.sharding import PartitionSpec as P

NORM_EPS = 1e-6
LEARN_RATE = 0.25
ROW_CONTRACT = (((0,), (0,)), ((), ()))
LAST_CONTRACT = (((1,), (1,)), ((), ()))


def rms_norm(state_f32):
    return state_f32 * lax.rsqrt(jnp.mean(state_f32 * state_f32, axis=-1, keepdims=True) + NORM_EPS)


def local_step(up_w, down_w, input_t, target_t, up_scale, down_scale):
    up_bf = up_w.astype(jnp.bfloat16)
    down_bf = down_w.astype(jnp.bfloat16)
    num_layers = up_w.shape[0]
    state = input_t
    saved = []
    for layer in range(num_layers):
        state_f32 = state.astype(jnp.float32)
        normed_f32, rms_back = jax.vjp(rms_norm, state_f32)
        normed = normed_f32.astype(jnp.bfloat16)
        pre_act = jnp.dot(normed, up_bf[layer], preferred_element_type=jnp.float32) * up_scale
        hidden_f32, gelu_back = jax.vjp(jax.nn.gelu, pre_act)
        hidden = hidden_f32.astype(jnp.bfloat16)
        branch = jnp.dot(hidden, down_bf[layer], preferred_element_type=jnp.float32) * down_scale
        state = (state_f32 + lax.psum(branch, "tp")).astype(jnp.bfloat16)
        saved.append((rms_back, normed, gelu_back, hidden))
    grad_state = (2.0 / input_t.shape[0]) * (state.astype(jnp.float32) - target_t.astype(jnp.float32))
    up_grads = []
    down_grads = []
    for layer in reversed(range(num_layers)):
        rms_back, normed, gelu_back, hidden = saved[layer]
        grad_out = (grad_state * down_scale).astype(jnp.bfloat16)
        down_grads.append(lax.dot_general(hidden, grad_out, ROW_CONTRACT, preferred_element_type=jnp.float32))
        grad_hidden = lax.dot_general(grad_out, down_bf[layer], LAST_CONTRACT, preferred_element_type=jnp.float32)
        grad_pre = (gelu_back(grad_hidden)[0] * up_scale).astype(jnp.bfloat16)
        up_grads.append(lax.dot_general(normed, grad_pre, ROW_CONTRACT, preferred_element_type=jnp.float32))
        if layer > 0:
            grad_norm = lax.psum(lax.dot_general(grad_pre, up_bf[layer], LAST_CONTRACT, preferred_element_type=jnp.float32), "tp")
            grad_state = grad_state + rms_back(grad_norm)[0]
    up_grad = jnp.stack(up_grads[::-1])
    down_grad = jnp.stack(down_grads[::-1])
    return up_bf, down_bf, up_grad, down_grad, state


def neighbour_routes(size):
    from_prev = [(source, (source + 1) % size) for source in range(size)]
    from_next = [(source, (source - 1) % size) for source in range(size)]
    return from_prev, from_next


def mix_terms(master, west, east, south, north):
    total = (master + west.astype(jnp.float32) + east.astype(jnp.float32)
             + south.astype(jnp.float32) + north.astype(jnp.float32))
    return total / 5.0


def solution(mesh):
    x_prev, x_next = neighbour_routes(mesh.shape["x"])
    y_prev, y_next = neighbour_routes(mesh.shape["y"])
    up_spec = P("x", "y", None, None, "tp")
    down_spec = P("x", "y", None, "tp", None)
    data_spec = P("x", "y")

    def run(w_up, w_down, inputs, targets):
        up_scale = w_up.shape[3] ** -0.5
        down_scale = w_up.shape[4] ** -0.5

        def device_fn(up_block, down_block, input_block, target_block):
            up_w = up_block[0, 0]
            down_w = down_block[0, 0]
            for step in range(input_block.shape[2]):
                up_bf, down_bf, up_grad, down_grad, state = local_step(
                    up_w, down_w, input_block[0, 0, step], target_block[0, 0, step], up_scale, down_scale)
                sent = (up_bf, down_bf)
                from_xm = lax.ppermute(sent, "x", x_prev)
                from_xp = lax.ppermute(sent, "x", x_next)
                from_ym = lax.ppermute(sent, "y", y_prev)
                from_yp = lax.ppermute(sent, "y", y_next)
                up_w = mix_terms(up_w, from_xm[0], from_xp[0], from_ym[0], from_yp[0]) - LEARN_RATE * up_grad
                down_w = mix_terms(down_w, from_xm[1], from_xp[1], from_ym[1], from_yp[1]) - LEARN_RATE * down_grad
            return up_w[None, None], down_w[None, None], state[None, None]

        return jax.shard_map(device_fn, mesh=mesh, in_specs=(up_spec, down_spec, data_spec, data_spec),
                             out_specs=(up_spec, down_spec, data_spec), check_vma=False)(w_up, w_down, inputs, targets)

    return run
```

profile of v0, /device:TPU:10, one launch (start us, length us, event | category | flops | bytes accessed | tf_op | source)
XLA Modules:
  0.0 2394.2 jit_solution(4396368682974686617)
XLA Ops:
  7.2 14.4 fusion.44
  21.7 0.6 copy-done.7
  22.3 36.7 %fusion.103 = f32[4096,2560]{1,0:T(8,128)} fusion(f32[4096]{0:T(1024)S(1)} %add_rsqrt_fusion.2, bf16[1,1,3,4096,1280]{4,3,2,1,0:T(8,128)(2,1)} %param.6, f32[1,1,1,1280,2560]{4,3,2,1,0:T(8,128)} %param.4), kind=kOutput, calls=%fused_computation.133 | convolution fusion | flops 26862551040 | bytes 65552384 | tf_op jit(solution)/shard_map/dot_general | solution.py:26
  59.0 47.4 %convolution_multiply_fusion.2 = f32[4096,1280]{1,0:T(8,128)} fusion(f32[1,1,1,2560,1280]{4,3,2,1,0:T(8,128)} %param.5, f32[4096,2560]{1,0:T(8,128)} %fusion.103), kind=kOutput, calls=%fused_computation.95 | convolution fusion | flops 26956922880 | bytes 76021760 | tf_op jit(solution)/shard_map/dot_general | solution.py:29
  106.4 8.3 bitcast_convert_fusion.1
  114.7 1.7 collective-permute-start.1
  116.5 1.5 collective-permute-start.2
  118.0 8.1 bitcast_convert_fusion
  126.1 1.7 collective-permute-start.7
  127.9 0.6 add_rsqrt_fusion.1
  128.5 443.4 %all-reduce.4.cloned.1.call-done = f32[4096,1280]{1,0:T(8,128)} async-done(((f32[4096,1280]{1,0:T(8,128)}), f32[4096,1280]{1,0:T(8,128)}) %all-reduce.4.cloned.1.call-update) | async-done | bytes 20971536 | tf_op jit(solution)/shard_map/psum | solution.py:30
  571.8 18.8 fusion.53
  590.6 65.2 %fusion.7.clone.5.clone.5 = bf16[4096,2560]{1,0:T(8,128)(2,1)} fusion(f32[4096,2560]{1,0:T(8,128)} %fusion.103, bf16[4096,1280]{1,0:T(8,128)(2,1)} %fusion.53, f32[1,1,1,2560,1280]{4,3,2,1,0:T(8,128)} %param.5), kind=kOutput, calls=%fused_computation.13.clone.clone.clone.clone.clone.clone.clone.clone.clone.2 | convolution fusion | flops 27077509120 | bytes 86507520 | tf_op jit(solution)/shard_map/dot_general | solution.py:39
  655.8 1.5 collective-permute-start.8
  657.3 44.7 %fusion.165 = (bf16[1,1280,2560]{2,1,0:T(8,128)(2,1)}, f32[1,1280,2560]{2,1,0:T(8,128)}) fusion(f32[4096]{0:T(1024)S(1)} %copy-done.8, bf16[1,1,3,4096,1280]{4,3,2,1,0:T(8,128)(2,1)} %param.6, bf16[1,1280,2560]{2,1,0:T(8,128)(2,1)} %collective-permute-done.2, bf16[1,1280,2560]{2,1,0:T(8,128)(2,1)} %collective-permute-done.1, ...), kind=kOutput, calls=%fused_computation.186 | convolution fusion | flops 26895319040 | bytes 83902464 | tf_op jit(solution)/shard_map/dot_general | solution.py:41
  702.0 35.4 %fusion.99 = f32[4096,2560]{1,0:T(8,128)} fusion(f32[4096]{0:T(1024)S(1)} %copy-done.5, bf16[1,1,3,4096,1280]{4,3,2,1,0:T(8,128)(2,1)} %param.6, bf16[1,1280,2560]{2,1,0:T(8,128)(2,1)} %get-tuple-element.10), kind=kOutput, calls=%fused_computation.131 | convolution fusion | flops 26859274240 | bytes 58998784 | tf_op jit(solution)/shard_map/dot_general | solution.py:26
  737.5 61.0 %collective-permute-done.8 = bf16[1,2560,1280]{2,1,0:T(8,128)(2,1)} collective-permute-done((bf16[1,2560,1280]{2,1,0:T(8,128)(2,1)}, bf16[1,2560,1280]{2,1,0:T(8,128)(2,1)}, u32[]{:S(2)}, u32[]{:S(2)}) %collective-permute-start.8) | collective-permute-done | bytes 6553632 | tf_op jit(solution)/shard_map/ppermute | solution.py:82
  798.5 51.0 %fusion.168 = (bf16[1,2560,1280]{2,1,0:T(8,128)(2,1)}, f32[1,2560,1280]{2,1,0:T(8,128)}) fusion(bf16[4096,1280]{1,0:T(8,128)(2,1)} %fusion.53, f32[4096,2560]{1,0:T(8,128)} %fusion.103, bf16[1,2560,1280]{2,1,0:T(8,128)(2,1)} %collective-permute-done.8, bf16[1,2560,1280]{2,1,0:T(8,128)(2,1)} %collective-permute-done.7, ...), kind=kOutput, calls=%fused_computation.187 | convolution fusion | flops 26984448000 | bytes 104857600 | tf_op jit(solution)/shard_map/dot_general | solution.py:38
  849.5 44.7 %convolution_multiply_fusion.1 = f32[4096,1280]{1,0:T(8,128)} fusion(bf16[1,2560,1280]{2,1,0:T(8,128)(2,1)} %get-tuple-element.12, f32[4096,2560]{1,0:T(8,128)} %fusion.99), kind=kOutput, calls=%fused_computation.94 | convolution fusion | flops 26953646080 | bytes 69468160 | tf_op jit(solution)/shard_map/dot_general | solution.py:29
  894.3 0.6 copy-done.2
  895.0 0.6 add_rsqrt_fusion
  895.6 1.7 collective-permute-start.13
  897.3 1.7 collective-permute-start.4
  899.1 1.5 collective-permute-start.5
  900.5 459.2 %all-reduce.6.cloned.1.call-done = f32[4096,1280]{1,0:T(8,128)} async-done(((f32[4096,1280]{1,0:T(8,128)}), f32[4096,1280]{1,0:T(8,128)}) %all-reduce.6.cloned.1.call-update) | async-done | bytes 20971536 | tf_op jit(solution)/shard_map/psum | solution.py:30
  1359.7 18.8 fusion.51
  1378.5 64.7 %fusion.15.clone.7 = bf16[4096,2560]{1,0:T(8,128)(2,1)} fusion(f32[4096,2560]{1,0:T(8,128)} %fusion.99, bf16[4096,1280]{1,0:T(8,128)(2,1)} %fusion.51, bf16[1,2560,1280]{2,1,0:T(8,128)(2,1)} %get-tuple-element.12), kind=kOutput, calls=%fused_computation.21.clone.clone.clone.clone.clone.2 | convolution fusion | flops 27074232320 | bytes 79953920 | tf_op jit(solution)/shard_map/dot_general | solution.py:39
  1443.1 35.9 %fusion.76 = f32[1280,2560]{1,0:T(8,128)} fusion(f32[4096]{0:T(1024)S(1)} %copy-done.6, bf16[1,1,3,4096,1280]{4,3,2,1,0:T(8,128)(2,1)} %param.6, bf16[4096,2560]{1,0:T(8,128)(2,1)} %fusion.15.clone.7), kind=kOutput, calls=%fused_computation.106 | convolution fusion | flops 26862551040 | bytes 44580864 | tf_op jit(solution)/shard_map/dot_general | solution.py:41
  1479.0 42.9 %convolution_multiply_fusion.4 = f32[2560,1280]{1,0:T(8,128)} fusion(bf16[4096,1280]{1,0:T(8,128)(2,1)} %fusion.51, f32[4096,2560]{1,0:T(8,128)} %fusion.99), kind=kOutput, calls=%fused_computation.103 | convolution fusion | flops 26951680000 | bytes 65536000 | tf_op jit(solution)/shard_map/dot_general | solution.py:38
  1522.0 1.5 collective-permute-start.14
  1523.5 17.7 fusion.163
  1541.2 35.4 %fusion.95 = f32[4096,2560]{1,0:T(8,128)} fusion(f32[4096]{0:T(1024)S(1)} %copy-done.3, bf16[1,1,3,4096,1280]{4,3,2,1,0:T(8,128)(2,1)} %param.6, bf16[1,1280,2560]{2,1,0:T(8,128)(2,1)} %get-tuple-element.8), kind=kOutput, calls=%fused_computation.129 | convolution fusion | flops 26859274240 | bytes 58998784 | tf_op jit(solution)/shard_map/dot_general | solution.py:26
  1576.7 88.0 %collective-permute-done.14 = bf16[1,2560,1280]{2,1,0:T(8,128)(2,1)} collective-permute-done((bf16[1,2560,1280]{2,1,0:T(8,128)(2,1)}, bf16[1,2560,1280]{2,1,0:T(8,128)(2,1)}, u32[]{:S(2)}, u32[]{:S(2)}) %collective-permute-start.14) | collective-permute-done | bytes 6553632 | tf_op jit(solution)/shard_map/ppermute | solution.py:82
  1664.6 20.9 fusion.161
  1685.5 2.7 copy-done.1
  1688.2 43.0 %convolution_multiply_fusion = f32[4096,1280]{1,0:T(8,128)} fusion(bf16[1,2560,1280]{2,1,0:T(8,128)(2,1)S(1)} %get-tuple-element.6, f32[4096,2560]{1,0:T(8,128)} %fusion.95), kind=kOutput, calls=%fused_computation.93 | convolution fusion | flops 26953646080 | bytes 69468160 | tf_op jit(solution)/shard_map/dot_general | solution.py:29
  1731.2 0.1 collective-permute-start.15
  1731.3 1.7 collective-permute-start.16
  1733.0 1.4 collective-permute-start.17
  1734.4 0.6 collective-permute-start.11
  1735.0 461.6 %all-reduce.8.cloned.1.call-done = f32[4096,1280]{1,0:T(8,128)} async-done(((f32[4096,1280]{1,0:T(8,128)}), f32[4096,1280]{1,0:T(8,128)}) %all-reduce.8.cloned.1.call-update) | async-done | bytes 20971536 | tf_op jit(solution)/shard_map/psum | solution.py:30
  2196.6 15.2 fusion.46
  2211.8 60.6 %fusion.23.clone.9 = bf16[4096,2560]{1,0:T(8,128)(2,1)} fusion(f32[4096,2560]{1,0:T(8,128)} %fusion.95, bf16[1,2560,1280]{2,1,0:T(8,128)(2,1)} %copy-done.1, bf16[4096,1280]{1,0:T(8,128)(2,1)} %fusion.46, bf16[1,1,3,4096,1280]{4,3,2,1,0:T(8,128)(2,1)} %param.7), kind=kOutput, calls=%fused_computation.29.clone.clone.clone.clone.clone.clone.clone.2 | convolution fusion | flops 27100446720 | bytes 90439680 | tf_op jit(solution)/shard_map/dot_general | solution.py:39
  2272.4 0.1 collective-permute-start.9
  2272.4 53.7 %convolution_multiply_fusion.3 = f32[2560,1280]{1,0:T(8,128)} fusion(bf16[4096,1280]{1,0:T(8,128)(2,1)} %fusion.46, bf16[1,1,3,4096,1280]{4,3,2,1,0:T(8,128)(2,1)} %param.7, f32[4096,2560]{1,0:T(8,128)} %fusion.95), kind=kOutput, calls=%fused_computation.102 | convolution fusion | flops 26977894400 | bytes 76021760 | tf_op jit(solution)/shard_map/dot_general | solution.py:38
  2326.2 17.1 fusion.91
  2343.2 2.4 collective-permute-done.9
  2345.6 41.7 %fusion.86 = f32[1,1,1,1280,2560]{4,3,2,1,0:T(8,128)} fusion(bf16[1,1280,2560]{2,1,0:T(8,128)(2,1)} %collective-permute-done.11, bf16[1,1280,2560]{2,1,0:T(8,128)(2,1)} %collective-permute-done.10, f32[1,1280,2560]{2,1,0:T(8,128)} %get-tuple-element.9, bf16[1,1280,2560]{2,1,0:T(8,128)(2,1)} %collective-permute-done.9, f32[4096]{0:T(1024)S(1)} %copy-done.4, ...), kind=kOutput, calls=%fused_computation.116 | convolution fusion | flops 26892042240 | bytes 77348864 | tf_op jit(solution)/shard_map/dot_general | solution.py:41
  (51 shorter events, 0.3 us)
Async XLA Ops:
  7.2 564.7 %all-reduce.4.cloned.1.call-start = ((), (), s32[]{:S(2)}) async-start(), calls=%async_computation | async-start | bytes 41943040 | tf_op jit(solution)/shard_map/psum | solution.py:30
  21.7 0.6 copy-start.7
  106.3 1253.4 %all-reduce.6.cloned.1.call-start = ((), (), s32[]{:S(2)}) async-start(), calls=%async_computation.1 | async-start | bytes 41943040 | tf_op jit(solution)/shard_map/psum | solution.py:30
  114.7 541.1 %collective-permute-start = (bf16[1,1280,2560]{2,1,0:T(8,128)(2,1)}, bf16[1,1280,2560]{2,1,0:T(8,128)(2,1)}, u32[]{:S(2)}, u32[]{:S(2)}) collective-permute-start(bf16[1,1280,2560]{2,1,0:T(8,128)(2,1)} %bitcast_convert_fusion.1), channel_id=1, source_target_pairs={{0,1},{1,2},{2,3},{3,0},{4,5},{5,6},{6,7},{7,4},{8,9},{9,10},{10,1... | collective-permute-start | bytes 19660808 | tf_op jit(solution)/shard_map/ppermute | solution.py:80
  114.7 542.6 %collective-permute-start.1 = (bf16[1,1280,2560]{2,1,0:T(8,128)(2,1)}, bf16[1,1280,2560]{2,1,0:T(8,128)(2,1)}, u32[]{:S(2)}, u32[]{:S(2)}) collective-permute-start(bf16[1,1280,2560]{2,1,0:T(8,128)(2,1)} %bitcast_convert_fusion.1), channel_id=1, source_target_pairs={{0,3},{1,0},{2,1},{3,2},{4,7},{5,4},{6,5},{7,6},{8,11},{9,8},{10,9... | collective-permute-start | bytes 19660808 | tf_op jit(solution)/shard_map/ppermute | solution.py:81
  116.5 540.9 %collective-permute-start.2 = (bf16[1,1280,2560]{2,1,0:T(8,128)(2,1)}, bf16[1,1280,2560]{2,1,0:T(8,128)(2,1)}, u32[]{:S(2)}, u32[]{:S(2)}) collective-permute-start(bf16[1,1280,2560]{2,1,0:T(8,128)(2,1)} %bitcast_convert_fusion.1), channel_id=1, source_target_pairs={{0,4},{4,0},{1,5},{5,1},{2,6},{6,2},{3,7},{7,3},{8,12},{12,8},{9,1... | collective-permute-start | bytes 19660808 | tf_op jit(solution)/shard_map/ppermute | solution.py:82
  126.1 611.3 %collective-permute-start.6 = (bf16[1,2560,1280]{2,1,0:T(8,128)(2,1)}, bf16[1,2560,1280]{2,1,0:T(8,128)(2,1)}, u32[]{:S(2)}, u32[]{:S(2)}) collective-permute-start(bf16[1,2560,1280]{2,1,0:T(8,128)(2,1)} %bitcast_convert_fusion), channel_id=1, source_target_pairs={{0,1},{1,2},{2,3},{3,0},{4,5},{5,6},{6,7},{7,4},{8,9},{9,10},{10,1... | collective-permute-start | bytes 19660808 | tf_op jit(solution)/shard_map/ppermute | solution.py:80
  126.1 611.3 %collective-permute-start.7 = (bf16[1,2560,1280]{2,1,0:T(8,128)(2,1)}, bf16[1,2560,1280]{2,1,0:T(8,128)(2,1)}, u32[]{:S(2)}, u32[]{:S(2)}) collective-permute-start(bf16[1,2560,1280]{2,1,0:T(8,128)(2,1)} %bitcast_convert_fusion), channel_id=1, source_target_pairs={{0,3},{1,0},{2,1},{3,2},{4,7},{5,4},{6,5},{7,6},{8,11},{9,8},{10,9... | collective-permute-start | bytes 19660808 | tf_op jit(solution)/shard_map/ppermute | solution.py:81
  590.6 66.7 %copy-start.8 = (f32[4096]{0:T(1024)S(1)}, f32[4096]{0:T(1024)}, u32[]{:S(2)}) copy-start(f32[4096]{0:T(1024)} %copy-done.7) | copy-start | bytes 49156
  655.8 46.2 %copy-start.5 = (f32[4096]{0:T(1024)S(1)}, f32[4096]{0:T(1024)}, u32[]{:S(2)}) copy-start(f32[4096]{0:T(1024)} %add_rsqrt_fusion.1) | copy-start | bytes 49156
  655.8 142.7 %collective-permute-start.8 = (bf16[1,2560,1280]{2,1,0:T(8,128)(2,1)}, bf16[1,2560,1280]{2,1,0:T(8,128)(2,1)}, u32[]{:S(2)}, u32[]{:S(2)}) collective-permute-start(bf16[1,2560,1280]{2,1,0:T(8,128)(2,1)} %bitcast_convert_fusion), channel_id=1, source_target_pairs={{0,4},{4,0},{1,5},{5,1},{2,6},{6,2},{3,7},{7,3},{8,12},{12,8},{9,1... | collective-permute-start | bytes 19660808 | tf_op jit(solution)/shard_map/ppermute | solution.py:82
  894.2 0.7 copy-start.2
  894.3 1302.4 %all-reduce.8.cloned.1.call-start = ((), (), s32[]{:S(2)}) async-start(), calls=%async_computation.2 | async-start | bytes 41943040 | tf_op jit(solution)/shard_map/psum | solution.py:30
  895.6 681.1 %collective-permute-start.12 = (bf16[1,2560,1280]{2,1,0:T(8,128)(2,1)}, bf16[1,2560,1280]{2,1,0:T(8,128)(2,1)}, u32[]{:S(2)}, u32[]{:S(2)}) collective-permute-start(bf16[1,2560,1280]{2,1,0:T(8,128)(2,1)} %get-tuple-element.12), channel_id=1, source_target_pairs={{0,1},{1,2},{2,3},{3,0},{4,5},{5,6},{6,7},{7,4},{8,9},{9,10},{10,1... | collective-permute-start | bytes 19660808 | tf_op jit(solution)/shard_map/ppermute | solution.py:80
  895.6 681.1 %collective-permute-start.13 = (bf16[1,2560,1280]{2,1,0:T(8,128)(2,1)}, bf16[1,2560,1280]{2,1,0:T(8,128)(2,1)}, u32[]{:S(2)}, u32[]{:S(2)}) collective-permute-start(bf16[1,2560,1280]{2,1,0:T(8,128)(2,1)} %get-tuple-element.12), channel_id=1, source_target_pairs={{0,3},{1,0},{2,1},{3,2},{4,7},{5,4},{6,5},{7,6},{8,11},{9,8},{10,9... | collective-permute-start | bytes 19660808 | tf_op jit(solution)/shard_map/ppermute | solution.py:81
  897.3 624.6 %collective-permute-start.3 = (bf16[1,1280,2560]{2,1,0:T(8,128)(2,1)}, bf16[1,1280,2560]{2,1,0:T(8,128)(2,1)}, u32[]{:S(2)}, u32[]{:S(2)}) collective-permute-start(bf16[1,1280,2560]{2,1,0:T(8,128)(2,1)} %get-tuple-element.10), channel_id=1, source_target_pairs={{0,1},{1,2},{2,3},{3,0},{4,5},{5,6},{6,7},{7,4},{8,9},{9,10},{10,1... | collective-permute-start | bytes 19660808 | tf_op jit(solution)/shard_map/ppermute | solution.py:80
  897.3 626.1 %collective-permute-start.4 = (bf16[1,1280,2560]{2,1,0:T(8,128)(2,1)}, bf16[1,1280,2560]{2,1,0:T(8,128)(2,1)}, u32[]{:S(2)}, u32[]{:S(2)}) collective-permute-start(bf16[1,1280,2560]{2,1,0:T(8,128)(2,1)} %get-tuple-element.10), channel_id=1, source_target_pairs={{0,3},{1,0},{2,1},{3,2},{4,7},{5,4},{6,5},{7,6},{8,11},{9,8},{10,9... | collective-permute-start | bytes 19660808 | tf_op jit(solution)/shard_map/ppermute | solution.py:81
  899.1 624.4 %collective-permute-start.5 = (bf16[1,1280,2560]{2,1,0:T(8,128)(2,1)}, bf16[1,1280,2560]{2,1,0:T(8,128)(2,1)}, u32[]{:S(2)}, u32[]{:S(2)}) collective-permute-start(bf16[1,1280,2560]{2,1,0:T(8,128)(2,1)} %get-tuple-element.10), channel_id=1, source_target_pairs={{0,4},{4,0},{1,5},{5,1},{2,6},{6,2},{3,7},{7,3},{8,12},{12,8},{9,1... | collective-permute-start | bytes 19660808 | tf_op jit(solution)/shard_map/ppermute | solution.py:82
  1378.5 64.7 %copy-start.6 = (f32[4096]{0:T(1024)S(1)}, f32[4096]{0:T(1024)}, u32[]{:S(2)}) copy-start(f32[4096]{0:T(1024)} %add_rsqrt_fusion.1) | copy-start | bytes 49156
  1443.1 80.3 %slice-start = ((s8[13107200]{0:T(1024)(128)(4,1)}), s8[4194304]{0:T(1024)(128)(4,1)S(1)}, s32[]{:S(2)}) async-start(s8[13107200]{0:T(1024)(128)(4,1)} %bitcast.178), calls=%async_computation.3 | async-start | bytes 8388608
  1443.1 80.3 %slice-start.1 = ((s8[13107200]{0:T(1024)(128)(4,1)}), s8[4194304]{0:T(1024)(128)(4,1)S(1)}, s32[]{:S(2)}) async-start(s8[13107200]{0:T(1024)(128)(4,1)} %bitcast.178), calls=%async_computation.4 | async-start | bytes 8388608
  1479.0 44.4 %slice-start.2 = ((s8[13107200]{0:T(1024)(128)(4,1)}), s8[4194304]{0:T(1024)(128)(4,1)S(1)}, s32[]{:S(2)}) async-start(s8[13107200]{0:T(1024)(128)(4,1)} %bitcast.178), calls=%async_computation.5 | async-start | bytes 8388608
  1479.0 44.4 %slice-start.3 = ((s8[13107200]{0:T(1024)(128)(4,1)}), s8[524288]{0:T(1024)(128)(4,1)S(1)}, s32[]{:S(2)}) async-start(s8[13107200]{0:T(1024)(128)(4,1)} %bitcast.178), calls=%async_computation.6 | async-start | bytes 1048576
  1522.0 142.7 %collective-permute-start.14 = (bf16[1,2560,1280]{2,1,0:T(8,128)(2,1)}, bf16[1,2560,1280]{2,1,0:T(8,128)(2,1)}, u32[]{:S(2)}, u32[]{:S(2)}) collective-permute-start(bf16[1,2560,1280]{2,1,0:T(8,128)(2,1)} %get-tuple-element.12), channel_id=1, source_target_pairs={{0,4},{4,0},{1,5},{5,1},{2,6},{6,2},{3,7},{7,3},{8,12},{12,8},{9,1... | collective-permute-start | bytes 19660808 | tf_op jit(solution)/shard_map/ppermute | solution.py:82
  1523.5 17.7 copy-start.3
  1685.5 2.7 copy-start.1
  1731.2 541.2 %collective-permute-start.15 = (bf16[1,2560,1280]{2,1,0:T(8,128)(2,1)}, bf16[1,2560,1280]{2,1,0:T(8,128)(2,1)}, u32[]{:S(2)}, u32[]{:S(2)}) collective-permute-start(bf16[1,2560,1280]{2,1,0:T(8,128)(2,1)} %copy-done.1), channel_id=1, source_target_pairs={{0,1},{1,2},{2,3},{3,0},{4,5},{5,6},{6,7},{7,4},{8,9},{9,10},{10,1... | collective-permute-start | bytes 19660808 | tf_op jit(solution)/shard_map/ppermute | solution.py:80
  1731.3 594.9 %collective-permute-start.16 = (bf16[1,2560,1280]{2,1,0:T(8,128)(2,1)}, bf16[1,2560,1280]{2,1,0:T(8,128)(2,1)}, u32[]{:S(2)}, u32[]{:S(2)}) collective-permute-start(bf16[1,2560,1280]{2,1,0:T(8,128)(2,1)} %copy-done.1), channel_id=1, source_target_pairs={{0,3},{1,0},{2,1},{3,2},{4,7},{5,4},{6,5},{7,6},{8,11},{9,8},{10,9... | collective-permute-start | bytes 19660808 | tf_op jit(solution)/shard_map/ppermute | solution.py:81
  1733.0 593.2 %collective-permute-start.17 = (bf16[1,2560,1280]{2,1,0:T(8,128)(2,1)}, bf16[1,2560,1280]{2,1,0:T(8,128)(2,1)}, u32[]{:S(2)}, u32[]{:S(2)}) collective-permute-start(bf16[1,2560,1280]{2,1,0:T(8,128)(2,1)} %copy-done.1), channel_id=1, source_target_pairs={{0,4},{4,0},{1,5},{5,1},{2,6},{6,2},{3,7},{7,3},{8,12},{12,8},{9,1... | collective-permute-start | bytes 19660808 | tf_op jit(solution)/shard_map/ppermute | solution.py:82
  1734.4 608.8 %collective-permute-start.10 = (bf16[1,1280,2560]{2,1,0:T(8,128)(2,1)}, bf16[1,1280,2560]{2,1,0:T(8,128)(2,1)}, u32[]{:S(2)}, u32[]{:S(2)}) collective-permute-start(bf16[1,1280,2560]{2,1,0:T(8,128)(2,1)} %get-tuple-element.8), channel_id=1, source_target_pairs={{0,3},{1,0},{2,1},{3,2},{4,7},{5,4},{6,5},{7,6},{8,11},{9,8},{10,9... | collective-permute-start | bytes 19660808 | tf_op jit(solution)/shard_map/ppermute | solution.py:81
  1734.4 608.8 %collective-permute-start.11 = (bf16[1,1280,2560]{2,1,0:T(8,128)(2,1)}, bf16[1,1280,2560]{2,1,0:T(8,128)(2,1)}, u32[]{:S(2)}, u32[]{:S(2)}) collective-permute-start(bf16[1,1280,2560]{2,1,0:T(8,128)(2,1)} %get-tuple-element.8), channel_id=1, source_target_pairs={{0,4},{4,0},{1,5},{5,1},{2,6},{6,2},{3,7},{7,3},{8,12},{12,8},{9,1... | collective-permute-start | bytes 19660808 | tf_op jit(solution)/shard_map/ppermute | solution.py:82
  2272.4 53.8 %copy-start = (f32[1,2560,1280]{2,1,0:T(8,128)S(1)}, f32[1,2560,1280]{2,1,0:T(8,128)}, u32[]{:S(2)}) copy-start(f32[1,2560,1280]{2,1,0:T(8,128)} %get-tuple-element.7) | copy-start | bytes 39321604
  2272.4 73.3 %collective-permute-start.9 = (bf16[1,1280,2560]{2,1,0:T(8,128)(2,1)}, bf16[1,1280,2560]{2,1,0:T(8,128)(2,1)}, u32[]{:S(2)}, u32[]{:S(2)}) collective-permute-start(bf16[1,1280,2560]{2,1,0:T(8,128)(2,1)} %get-tuple-element.8), channel_id=1, source_target_pairs={{0,1},{1,2},{2,3},{3,0},{4,5},{5,6},{6,7},{7,4},{8,9},{9,10},{10,1... | collective-permute-start | bytes 19660808 | tf_op jit(solution)/shard_map/ppermute | solution.py:80
  2326.2 19.5 copy-start.4
Sparse Core Ops, SparseCore 0:
  106.5 465.3 all-reduce.3
  894.4 465.2 all-reduce.5
  1731.3 465.2 all-reduce.7
where the time goes:
time: 2400 us; the launch traced here: 2390 us
  waiting for transfers between devices  1520 us (63%)
  matrix products  703 us (29%)
  other arithmetic  140 us (6%)
    psum x3, waiting for transfers between devices, local_step(): state = (state_f32 + lax.psum(branch, 'tp')).astype(jnp.bfloat16)  1360 us
    dot_general x3, matrix products, local_step(): lax.dot_general(grad_out, down_bf[layer], LAST_CONTRACT, preferred_elemen...  190 us
    ppermute x6, waiting for transfers between devices, device_fn(): from_ym = lax.ppermute(sent, 'y', y_prev)  149 us
    dot_general x3, matrix products, local_step(): lax.dot_general(hidden, grad_out, ROW_CONTRACT, preferred_element_type=jn...  148 us
    dot_general x3, matrix products, local_step(): jnp.dot(hidden, down_bf[layer], preferred_element_type=jnp.float32)  135 us
    dot_general x3, matrix products, local_step(): lax.dot_general(normed, grad_pre, ROW_CONTRACT, preferred_element_type=jn...  122 us
    dot_general x3, matrix products, local_step(): jnp.dot(normed, up_bf[layer], preferred_element_type=jnp.float32) * up_scale  108 us
  transfers between devices with their start and end apart: 21, of which 6 were waited for; matrix products, arithmetic and copies ran while one was open for 23% of the time, Pallas kernels for 0%

commit v1 on v0

v1 whole, which is shorter than its diff:
```python
import functools
import math

import jax
import jax.numpy as jnp
from jax import lax
from jax.experimental import pallas as pl
from jax.experimental.pallas import tpu as pltpu
from jax.sharding import PartitionSpec as P

NORM_EPS = 1e-6
LEARN_RATE = 0.25
TILE = 512
ROWS = 512
CHUNK = 32
GELU_C = math.sqrt(2.0 / math.pi)
GELU_A = 0.044715
BF = jnp.bfloat16
F32 = jnp.float32
MESH = pl.DeviceIdType.MESH
NT_DIMS = (((1,), (1,)), ((), ()))
MATE, FAR, SIDE, DEEP = 0, 1, 2, 3


def dot_nt(a, b):
    return lax.dot_general(a, b, NT_DIMS, preferred_element_type=F32)


def dot_nn(a, b):
    return jnp.dot(a, b, preferred_element_type=F32)


def kernel(steps, num_rows, hidden, up_scale, down_scale,
           inp, tgt, w1, w2, wb0,
           o1, o2, hb, wb, hs, gm, gf, gy, zr, xin,
           r_v, go_v, v, wt, gb, ob, st,
           s_snd, s_rcv, f_snd, h_snd, h_rcv, x_snd, x_rcv,
           l_wt, l_own, l_g, l_st, l_out):
    half_rows = num_rows // 2
    nt = hidden // TILE
    nb = num_rows // ROWS
    hb_n = half_rows // ROWS
    bufs = (gm, gf, gy, zr)

    ix, iy, iz = lax.axis_index("x"), lax.axis_index("y"), lax.axis_index("tp")
    core = lax.rem(ix, 2)
    host = core == iz
    guest = core != iz
    mate_x = ix + 1 - 2 * core
    mate = {"x": mate_x, "y": iy, "tp": iz}
    far = {"x": 3 - ix, "y": iy, "tp": iz}
    side = {"x": ix, "y": 1 - iy, "tp": iz}
    deep = {"x": ix, "y": iy, "tp": 1 - iz}
    diag = {"x": mate_x, "y": iy, "tp": 1 - iz}
    peers = (mate, far, side, deep)

    barrier = pltpu.get_barrier_semaphore()
    for peer in (mate, far, side, deep, diag):
        pl.semaphore_signal(barrier, inc=1, device_id=peer, device_id_type=MESH)
    pl.semaphore_wait(barrier, 5)

    def tile_rows(j):
        return pl.ds(pl.multiple_of(j * TILE, TILE), TILE)

    def block(m):
        return pl.ds(pl.multiple_of(m * ROWS, ROWS), ROWS)

    def tile_copy(kind, t, j, src):
        return pltpu.make_async_remote_copy(
            src_ref=src.at[:, tile_rows(j)], dst_ref=bufs[kind].at[t, :, tile_rows(j)],
            send_sem=s_snd.at[kind, t, j], recv_sem=s_rcv.at[kind, t, j],
            device_id=peers[kind], device_id_type=MESH)

    def send_tile(t, j, src):
        @pl.when(guest)
        def _():
            tile_copy(DEEP, t, j, src).start()
        for kind in (MATE, FAR, SIDE):
            tile_copy(kind, t, j, src).start()

    def forward_copy(t, j):
        return pltpu.make_async_remote_copy(
            src_ref=zr.at[t, :, tile_rows(j)], dst_ref=zr.at[t, :, tile_rows(j)],
            send_sem=f_snd.at[t, j], recv_sem=s_rcv.at[DEEP, t, j],
            device_id=mate, device_id_type=MESH)

    def half_copy(t):
        other = pl.ds(pl.multiple_of((1 - core) * half_rows, half_rows), half_rows)
        return pltpu.make_async_remote_copy(
            src_ref=inp.at[t, other], dst_ref=xin.at[t], send_sem=x_snd.at[t], recv_sem=x_rcv.at[t],
            device_id=mate, device_id_type=MESH)

    def rows_of(half, m):
        return pl.ds(pl.multiple_of(half * half_rows + m * ROWS, ROWS), ROWS)

    def h_host_copy(t, m):
        return pltpu.make_async_remote_copy(
            src_ref=hb.at[t, rows_of(core, m)], dst_ref=hb.at[t, rows_of(core, m)],
            send_sem=h_snd.at[0, t, m], recv_sem=h_rcv.at[core, t, m], device_id=deep, device_id_type=MESH)

    def h_guest_copy(which, t, m):
        return pltpu.make_async_remote_copy(
            src_ref=hs.at[t, block(m)], dst_ref=hb.at[t, rows_of(core, m)],
            send_sem=h_snd.at[which, t, m], recv_sem=h_rcv.at[core, t, m],
            device_id=(diag, mate)[which], device_id_type=MESH)

    def h_wait(t, half, m):
        pltpu.make_async_remote_copy(
            src_ref=hb.at[t, rows_of(half, m)], dst_ref=hb.at[t, rows_of(half, m)],
            send_sem=h_snd.at[0, t, m], recv_sem=h_rcv.at[half, t, m], device_id=deep, device_id_type=MESH).wait_recv()

    def own_tile(t, j, slot):
        @pl.when(t == 0)
        def _():
            pltpu.make_async_copy(wb0.at[:, tile_rows(j)], wt.at[slot], l_wt.at[slot]).start()

        @pl.when(t > 0)
        def _():
            pltpu.make_async_copy(wb.at[t - 1, :, tile_rows(j)], wt.at[slot], l_wt.at[slot]).start()

    def wait_tile(slot):
        pltpu.make_async_copy(wb0.at[:, tile_rows(0)], wt.at[slot], l_wt.at[slot]).wait()

    def stage(src, slot):
        return pltpu.make_async_copy(src, st.at[slot], l_st.at[slot])

    def stage_wait(slot):
        stage(inp.at[0, block(0)], slot).wait()

    def stage_fwd_rows(t, m, slot):
        @pl.when(host)
        def _():
            stage(inp.at[t, rows_of(core, m)], slot).start()

        @pl.when(guest)
        def _():
            stage(xin.at[t, block(m)], slot).start()

    def norm_block(slot, m):
        def body(c, carry):
            x = st[slot, pl.ds(pl.multiple_of(c * CHUNK, CHUNK), CHUNK), :].astype(F32)
            inv = lax.rsqrt(jnp.mean(x * x, axis=-1, keepdims=True) + NORM_EPS)
            r_v[pl.ds(pl.multiple_of(m * ROWS + c * CHUNK, CHUNK), CHUNK), :] = (x * inv).astype(BF)
            return carry
        lax.fori_loop(0, ROWS // CHUNK, body, 0)

    def zero(first, count):
        def body(c, carry):
            v[pl.ds(pl.multiple_of(first + c * CHUNK, CHUNK), CHUNK), :] = jnp.zeros((CHUNK, v.shape[1]), F32)
            return carry
        lax.fori_loop(0, count // CHUNK, body, 0)

    @pl.when(host)
    def _():
        half_copy(0).start()

    def first_sends(j, carry):
        send_tile(0, j, wb0)
        return carry
    lax.fori_loop(0, nt, first_sends, 0)

    @pl.when(host)
    def _():
        def body(t, carry):
            half_copy(t).start()
            return carry
        lax.fori_loop(1, steps, body, 0)

    def step(t, carry):
        @pl.when(guest)
        def _():
            half_copy(t).wait_recv()
        stage_fwd_rows(t, 0, 0)
        for m in range(hb_n):
            if m + 1 < hb_n:
                stage_fwd_rows(t, m + 1, (m + 1) % 2)
            stage_wait(m % 2)
            norm_block(m % 2, m)
        zero(0, half_rows)

        def start_tile(i, slot):
            j = lax.rem(i, nt)

            @pl.when(jnp.logical_and(i < nt, host))
            def _():
                own_tile(t, j, slot)

            @pl.when(jnp.logical_and(i < nt, guest))
            def _():
                tile_copy(MATE, t, j, wb0).wait_recv()
                pltpu.make_async_copy(gm.at[t, :, tile_rows(j)], wt.at[slot], l_wt.at[slot]).start()

            @pl.when(i >= nt)
            def _():
                tile_copy(DEEP, t, j, wb0).wait_recv()
                pltpu.make_async_copy(zr.at[t, :, tile_rows(j)], wt.at[slot], l_wt.at[slot]).start()

            @pl.when(jnp.logical_and(i >= nt, host))
            def _():
                forward_copy(t, j).start()

        start_tile(jnp.int32(0), 0)

        def fwd_tile(i, carry):
            slot = lax.rem(i, 2)

            @pl.when(i + 1 < 2 * nt)
            def _():
                start_tile(i + 1, 1 - slot)
            wait_tile(slot)

            def fwd_block(m, carry):
                x = dot_nt(r_v[block(m), :], wt[slot, 0]) * up_scale
                cdf = 0.5 + 0.5 * jnp.tanh(x * (GELU_C + (GELU_C * GELU_A) * (x * x)))
                a = (x * cdf).astype(BF)
                v[block(m), :] += dot_nn(a, wt[slot, 1])
                return carry
            lax.fori_loop(0, hb_n, fwd_block, 0)
            return carry
        lax.fori_loop(0, 2 * nt, fwd_tile, 0)

        stage_fwd_rows(t, 0, 0)
        for m in range(hb_n):
            slot = m % 2
            if m + 1 < hb_n:
                stage_fwd_rows(t, m + 1, 1 - slot)
            stage_wait(slot)

            def add_rows(c, carry):
                rows = pl.ds(pl.multiple_of(c * CHUNK, CHUNK), CHUNK)
                acc = v[pl.ds(pl.multiple_of(m * ROWS + c * CHUNK, CHUNK), CHUNK), :]
                ob[slot, rows, :] = (st[slot, rows, :].astype(F32) + acc * down_scale).astype(BF)
                return carry
            lax.fori_loop(0, ROWS // CHUNK, add_rows, 0)

            @pl.when(host)
            def _():
                out = pltpu.make_async_copy(ob.at[slot], hb.at[t, rows_of(core, m)], l_out.at[2])
                out.start()
                out.wait()
                h_host_copy(t, m).start()

            @pl.when(guest)
            def _():
                out = pltpu.make_async_copy(ob.at[slot], hs.at[t, block(m)], l_out.at[2])
                out.start()
                out.wait()
                h_guest_copy(0, t, m).start()
                h_guest_copy(1, t, m).start()

        stage(inp.at[t, block(0)], 0).start()
        for m in range(nb):
            if m + 1 < nb:
                stage(inp.at[t, block(m + 1)], (m + 1) % 2).start()
            stage_wait(m % 2)
            norm_block(m % 2, m)

        own_tile(t, jnp.int32(0), 0)

        def go_piece(i, carry):
            m = i // 2
            half = lax.rem(core + i, 2)
            rows = rows_of(half, m)
            stage(tgt.at[t, rows], 1).start()

            @pl.when(jnp.logical_or(guest, half != core))
            def _():
                h_wait(t, half, m)
            stage(hb.at[t, rows], 0).start()
            stage_wait(1)
            stage_wait(0)

            def body(c, carry):
                part = pl.ds(pl.multiple_of(c * CHUNK, CHUNK), CHUNK)
                diff = st[0, part, :].astype(F32) - st[1, part, :].astype(F32)
                g = ((2.0 / num_rows) * diff) * down_scale
                go_v[pl.ds(pl.multiple_of(half * half_rows + m * ROWS + c * CHUNK, CHUNK), CHUNK), :] = g.astype(BF)
                return carry
            lax.fori_loop(0, ROWS // CHUNK, body, 0)
            return carry
        lax.fori_loop(0, nb, go_piece, 0)

        def load_own(j):
            @pl.when(t == 0)
            def _():
                pltpu.make_async_copy(w1.at[tile_rows(j)], v.at[pl.ds(2 * TILE, TILE)], l_own.at[0]).start()
                pltpu.make_async_copy(w2.at[tile_rows(j)], v.at[pl.ds(3 * TILE, TILE)], l_own.at[1]).start()

            @pl.when(t > 0)
            def _():
                pltpu.make_async_copy(o1.at[tile_rows(j)], v.at[pl.ds(2 * TILE, TILE)], l_own.at[0]).start()
                pltpu.make_async_copy(o2.at[tile_rows(j)], v.at[pl.ds(3 * TILE, TILE)], l_own.at[1]).start()

        def bwd_tile(j, carry):
            slot = lax.rem(j, 2)

            @pl.when(j + 1 < nt)
            def _():
                own_tile(t, j + 1, 1 - slot)
            load_own(j)
            zero(0, 2 * TILE)
            wait_tile(slot)

            def bwd_block(m, carry):
                r_m = r_v[block(m), :]
                go_m = go_v[block(m), :]
                x = dot_nt(wt[slot, 0], r_m) * up_scale
                dh = dot_nt(wt[slot, 1], go_m)
                x2 = x * x
                th = jnp.tanh(x * (GELU_C + (GELU_C * GELU_A) * x2))
                cdf = 0.5 + 0.5 * th
                slope = cdf + (x * (0.5 * GELU_C + (1.5 * GELU_C * GELU_A) * x2)) * (1.0 - th * th)
                a = (x * cdf).astype(BF)
                dp = ((dh * slope) * up_scale).astype(BF)
                v[pl.ds(TILE, TILE), :] += dot_nn(a, go_m)
                v[pl.ds(0, TILE), :] += dot_nn(dp, r_m)

                @pl.when(m == nb - 2)
                def _():
                    @pl.when(host)
                    def _():
                        tile_copy(MATE, t, j, wb0).wait_recv()
                    tile_copy(FAR, t, j, wb0).wait_recv()
                    tile_copy(SIDE, t, j, wb0).wait_recv()
                    for kind in (MATE, FAR, SIDE):
                        pltpu.make_async_copy(bufs[kind].at[t, :, tile_rows(j)], gb.at[kind], l_g.at[kind]).start()
                return carry
            lax.fori_loop(0, nb, bwd_block, 0)

            for kind in (MATE, FAR, SIDE):
                pltpu.make_async_copy(bufs[kind].at[t, :, tile_rows(j)], gb.at[kind], l_g.at[kind]).wait()
            outs = (o1, o2)
            for w in range(2):
                own_at = (2 + w) * TILE
                pltpu.make_async_copy(outs[w].at[tile_rows(j)], v.at[pl.ds(own_at, TILE)], l_own.at[w]).wait()

                def update(c, carry):
                    part = pl.ds(pl.multiple_of(c * CHUNK, CHUNK), CHUNK)
                    own = pl.ds(pl.multiple_of(own_at + c * CHUNK, CHUNK), CHUNK)
                    grad = v[pl.ds(pl.multiple_of(w * TILE + c * CHUNK, CHUNK), CHUNK), :]
                    total = (v[own, :] + gb[MATE, w, part, :].astype(F32) + gb[FAR, w, part, :].astype(F32)
                             + 2.0 * gb[SIDE, w, part, :].astype(F32))
                    new = total * 0.2 - LEARN_RATE * grad
                    v[own, :] = new
                    ob[w, part, :] = new.astype(BF)
                    return carry
                lax.fori_loop(0, TILE // CHUNK, update, 0)
                pltpu.make_async_copy(v.at[pl.ds(own_at, TILE)], outs[w].at[tile_rows(j)], l_out.at[w]).start()

            @pl.when(t < steps - 1)
            def _():
                copy = pltpu.make_async_copy(ob, wb.at[t, :, tile_rows(j)], l_out.at[2])
                copy.start()
                copy.wait()
                send_tile(t + 1, j, wb.at[t])
            for w in range(2):
                pltpu.make_async_copy(v.at[pl.ds((2 + w) * TILE, TILE)], outs[w].at[tile_rows(j)], l_out.at[w]).wait()
            return carry
        lax.fori_loop(0, nt, bwd_tile, 0)
        return carry
    lax.fori_loop(0, steps, step, 0)

    def drain(t, carry):
        def body(j, carry):
            for kind in (MATE, FAR, SIDE):
                tile_copy(kind, t, j, wb0).wait_send()

            @pl.when(guest)
            def _():
                tile_copy(DEEP, t, j, wb0).wait_send()

            @pl.when(host)
            def _():
                forward_copy(t, j).wait_send()
            return carry
        lax.fori_loop(0, nt, body, 0)

        def h_body(m, carry):
            @pl.when(host)
            def _():
                h_host_copy(t, m).wait_send()

            @pl.when(guest)
            def _():
                h_guest_copy(0, t, m).wait_send()
                h_guest_copy(1, t, m).wait_send()
            return carry
        lax.fori_loop(0, hb_n, h_body, 0)

        @pl.when(host)
        def _():
            half_copy(t).wait_send()
        return carry
    lax.fori_loop(0, steps, drain, 0)


def train(inputs, targets, w1, w2, wb0):
    steps, num_rows, model = inputs.shape
    hidden = w1.shape[0]
    nt = hidden // TILE
    half_rows = num_rows // 2
    hb_n = half_rows // ROWS
    body = functools.partial(kernel, steps, num_rows, hidden, model ** -0.5, (2 * hidden) ** -0.5)
    shard = jax.ShapeDtypeStruct((steps, 2, hidden, model), BF)
    out_shape = (
        jax.ShapeDtypeStruct(w1.shape, F32), jax.ShapeDtypeStruct(w2.shape, F32),
        jax.ShapeDtypeStruct(inputs.shape, BF),
        jax.ShapeDtypeStruct((steps - 1, 2, hidden, model), BF),
        jax.ShapeDtypeStruct((steps, half_rows, model), BF),
        shard, shard, shard, shard,
        jax.ShapeDtypeStruct((steps, half_rows, model), BF))
    any_spec = pl.BlockSpec(memory_space=pl.ANY)
    dma = pltpu.SemaphoreType.DMA
    flops = steps * 12 * num_rows * hidden * model
    return pl.pallas_call(
        body, out_shape=out_shape, in_specs=[any_spec] * 5, out_specs=[any_spec] * len(out_shape),
        scratch_shapes=[
            pltpu.VMEM((num_rows, model), BF), pltpu.VMEM((num_rows, model), BF),
            pltpu.VMEM((half_rows, model), F32),
            pltpu.VMEM((2, 2, TILE, model), BF), pltpu.VMEM((3, 2, TILE, model), BF),
            pltpu.VMEM((2, TILE, model), BF), pltpu.VMEM((2, ROWS, model), BF),
            dma((4, steps, nt)), dma((4, steps, nt)), dma((steps, nt)),
            dma((2, steps, hb_n)), dma((2, steps, hb_n)), dma((steps,)), dma((steps,)),
            dma((2,)), dma((2,)), dma((3,)), dma((2,)), dma((3,)),
        ],
        compiler_params=pltpu.CompilerParams(collective_id=0, has_side_effects=True, vmem_limit_bytes=64000000),
        cost_estimate=pl.CostEstimate(flops=flops, bytes_accessed=600000000, transcendentals=0),
        name="steps",
    )(inputs, targets, w1, w2, wb0)


def solution(mesh):
    up_spec = P("x", "y", None, None, "tp")
    down_spec = P("x", "y", None, "tp", None)
    data_spec = P("x", "y")

    def device_fn(up_block, down_block, input_block, target_block):
        w1 = up_block[0, 0, 0].T
        w2 = down_block[0, 0, 0]
        wb0 = jnp.stack([w1.astype(BF), w2.astype(BF)])
        outs = train(input_block[0, 0], target_block[0, 0], w1, w2, wb0)
        return outs[0].T[None, None, None], outs[1][None, None, None], outs[2][-1][None, None]

    def run(w_up, w_down, inputs, targets):
        return jax.shard_map(device_fn, mesh=mesh, in_specs=(up_spec, down_spec, data_spec, data_spec),
                             out_specs=(up_spec, down_spec, data_spec), check_vma=False)(w_up, w_down, inputs, targets)

    return run
```

time: 2400 us -> 1130 us (0.47)
  waiting for transfers between devices: 1520 us -> 0 us
  Pallas kernels: 0 us -> 1060 us
  matrix products: 703 us -> 0 us
  other arithmetic: 140 us -> 27.1 us
  local copies, waits for them, and re-layouts: 3.94 us -> 47.1 us
    psum x3 -> x0, waiting for transfers between devices: 1360 us -> none  [local_step(): state = (state_f32 + lax.psum(branch, 'tp')).astype(jnp.bfloat16)]
    pallas_call x0 -> x1, Pallas kernels: none -> 1060 us  [train(): pl.pallas_call(body, out_shape=out_shape, in_specs=[any_spec] * 5, out_sp...]
    dot_general x15 -> x0, matrix products: 703 us -> none  [the longest x3 190 us: local_step(): lax.dot_general(grad_out, down_bf[layer], LAST_CONTRACT, preferred_elemen...]
    ppermute x18 -> x0, waiting for transfers between devices: 151 us -> none  [the longest x6 149 us: device_fn(): from_ym = lax.ppermute(sent, 'y', y_prev)]
    convert_element_type x7 -> x1, other arithmetic: 108 us -> 8.15 us  [device_fn(): wb0 = jnp.stack([w1.astype(BF), w2.astype(BF)])]
    unnamed x26 -> x3, local copies, waits for them, and re-layouts: 3.94 us -> 38.3 us
  transfers between devices with their start and end apart: 21 -> 0, of which waited for: 6 -> 0; matrix products, arithmetic and copies ran while one was open for 23% -> 0% of each run, Pallas kernels for 0% -> 0%
where the time goes in v1:
time: 1130 us
  Pallas kernels  1060 us (94%)
  local copies, waits for them, and re-layouts  47.1 us (4%)
  other arithmetic  27.1 us (2%)
    pallas_call x1, Pallas kernels, train(): pl.pallas_call(body, out_shape=out_shape, in_specs=[any_spec] * 5, out_sp...  1060 us
    unnamed x3, local copies, waits for them, and re-layouts  38.3 us

profile of v1, /device:TPU:10, one launch (start us, length us, event | category | flops | bytes accessed | tf_op | source)
XLA Modules:
  0.0 1131.4 jit_solution(8616842180028790710)
XLA Ops:
  0.6 8.2 convert_bitcast_fusion
  8.8 13.9 %copy.7 = f32[1,1,1,1280,2560]{3,4,2,1,0:T(8,128)} copy(f32[1,1,1,1280,2560]{4,3,2,1,0:T(8,128)} %param.4) | data formatting | bytes 26214400 | tf_op args[0]
  22.7 8.1 convert_bitcast_fusion.1
  30.8 10.9 pad_maximum_fusion.wb0
  41.6 1056.6 %steps.1 = (f32[2560,1280]{1,0:T(8,128)}, f32[2560,1280]{1,0:T(8,128)}, bf16[3,4096,1280]{2,1,0:T(8,128)(2,1)}, bf16[2,2,2560,1280]{3,2,1,0:T(8,128)(2,1)}, bf16...) custom-call(bf16[3,4096,1280]{2,1,0:T(8,128)(2,1)} %bitcast.21, ...), custom_call_target="tpu_custom_call" | custom-call | flops 483183820800 | bytes 600000000 | tf_op jit(solution)/shard_map/steps/pallas_call | solution.py:415
  1098.2 13.9 %copy.8 = f32[1,1,1,1280,2560]{4,3,2,1,0:T(8,128)} copy(f32[1,1,1,1280,2560]{3,4,2,1,0:T(8,128)} %bitcast.20) | data formatting | bytes 26214400
  1112.1 8.7 slice_bitcast_fusion
  1120.9 10.5 copy.10

commit v2 on v1

v2 whole, which is shorter than its diff:
```python
import functools
import math

import jax
import jax.numpy as jnp
from jax import lax
from jax.experimental import pallas as pl
from jax.experimental.pallas import tpu as pltpu
from jax.sharding import PartitionSpec as P

NORM_EPS = 1e-6
LEARN_RATE = 0.25
TILE = 512
ROWS = 512
CHUNK = 32
GELU_C = math.sqrt(2.0 / math.pi)
GELU_A = 0.044715
BF = jnp.bfloat16
F32 = jnp.float32
MESH = pl.DeviceIdType.MESH
NT_DIMS = (((1,), (1,)), ((), ()))
MATE, FAR, SIDE, DEEP = 0, 1, 2, 3


def dot_nt(a, b):
    return lax.dot_general(a, b, NT_DIMS, preferred_element_type=F32)


def dot_nn(a, b):
    return jnp.dot(a, b, preferred_element_type=F32)


def kernel(steps, num_rows, hidden, up_scale, down_scale,
           inp, tgt, w1, w2,
           o1, o2, hb, wb, hs, rn, gm, gf, gy, zr, xin,
           acc, wall, own, gb, ob, st, rb,
           s_snd, s_rcv, f_snd, h_snd, h_rcv, x_snd, x_rcv,
           l_wt, l_own, l_g, l_st, l_tg, l_rb, l_out, l_of):
    half_rows = num_rows // 2
    nt = hidden // TILE
    nb = num_rows // ROWS
    hb_n = half_rows // ROWS
    bufs = (gm, gf, gy, zr)

    ix, iy, iz = lax.axis_index("x"), lax.axis_index("y"), lax.axis_index("tp")
    core = lax.rem(ix, 2)
    host = core == iz
    guest = core != iz
    mate_x = ix + 1 - 2 * core
    mate = {"x": mate_x, "y": iy, "tp": iz}
    far = {"x": 3 - ix, "y": iy, "tp": iz}
    side = {"x": ix, "y": 1 - iy, "tp": iz}
    deep = {"x": ix, "y": iy, "tp": 1 - iz}
    diag = {"x": mate_x, "y": iy, "tp": 1 - iz}
    peers = (mate, far, side, deep)

    barrier = pltpu.get_barrier_semaphore()
    for peer in (mate, far, side, deep, diag):
        pl.semaphore_signal(barrier, inc=1, device_id=peer, device_id_type=MESH)
    pl.semaphore_wait(barrier, 5)

    def tile_rows(j):
        return pl.ds(pl.multiple_of(j * TILE, TILE), TILE)

    def block(m):
        return pl.ds(pl.multiple_of(m * ROWS, ROWS), ROWS)

    def tile_copy(kind, t, j, src):
        return pltpu.make_async_remote_copy(
            src_ref=src.at[:, tile_rows(j)], dst_ref=bufs[kind].at[t, :, tile_rows(j)],
            send_sem=s_snd.at[kind, t, j], recv_sem=s_rcv.at[kind, t, j],
            device_id=peers[kind], device_id_type=MESH)

    def send_tile(t, j, src):
        @pl.when(guest)
        def _():
            tile_copy(DEEP, t, j, src).start()
        for kind in (MATE, FAR, SIDE):
            tile_copy(kind, t, j, src).start()

    def forward_copy(t, j):
        return pltpu.make_async_remote_copy(
            src_ref=zr.at[t, :, tile_rows(j)], dst_ref=zr.at[t, :, tile_rows(j)],
            send_sem=f_snd.at[t, j], recv_sem=s_rcv.at[DEEP, t, j],
            device_id=mate, device_id_type=MESH)

    def half_copy(t):
        other = pl.ds(pl.multiple_of((1 - core) * half_rows, half_rows), half_rows)
        return pltpu.make_async_remote_copy(
            src_ref=inp.at[t, other], dst_ref=xin.at[t], send_sem=x_snd.at[t], recv_sem=x_rcv.at[t],
            device_id=mate, device_id_type=MESH)

    def rows_of(half, m):
        return pl.ds(pl.multiple_of(half * half_rows + m * ROWS, ROWS), ROWS)

    def h_host_copy(t, m):
        return pltpu.make_async_remote_copy(
            src_ref=hb.at[t, rows_of(core, m)], dst_ref=hb.at[t, rows_of(core, m)],
            send_sem=h_snd.at[0, t, m], recv_sem=h_rcv.at[core, t, m], device_id=deep, device_id_type=MESH)

    def h_guest_copy(which, t, m):
        return pltpu.make_async_remote_copy(
            src_ref=hs.at[t, block(m)], dst_ref=hb.at[t, rows_of(core, m)],
            send_sem=h_snd.at[which, t, m], recv_sem=h_rcv.at[core, t, m],
            device_id=(diag, mate)[which], device_id_type=MESH)

    def h_wait(t, half, m):
        pltpu.make_async_remote_copy(
            src_ref=hb.at[t, rows_of(half, m)], dst_ref=hb.at[t, rows_of(half, m)],
            send_sem=h_snd.at[0, t, m], recv_sem=h_rcv.at[half, t, m], device_id=deep, device_id_type=MESH).wait_recv()

    def own_tile(t, j, slot):
        pltpu.make_async_copy(wb.at[t, :, tile_rows(j)], wall.at[slot], l_wt.at[slot]).start()

    def wait_tile(slot):
        pltpu.make_async_copy(wb.at[0, :, tile_rows(0)], wall.at[slot], l_wt.at[slot]).wait()

    def stage(src, slot):
        return pltpu.make_async_copy(src, st.at[slot], l_st.at[slot])

    def stage_wait(slot):
        stage(inp.at[0, block(0)], slot).wait()

    def stage_fwd_rows(t, m, slot):
        @pl.when(host)
        def _():
            stage(inp.at[t, rows_of(core, m)], slot).start()

        @pl.when(guest)
        def _():
            stage(xin.at[t, block(m)], slot).start()

    def norm_rows(src, dst, base):
        def body(c, carry):
            part = pl.ds(pl.multiple_of(c * CHUNK, CHUNK), CHUNK)
            x = src[part, :].astype(F32)
            inv = lax.rsqrt(jnp.mean(x * x, axis=-1, keepdims=True) + NORM_EPS)
            dst[pl.ds(pl.multiple_of(base + c * CHUNK, CHUNK), CHUNK), :] = (x * inv).astype(BF)
            return carry
        lax.fori_loop(0, ROWS // CHUNK, body, 0, unroll=4)

    def zero(first, count):
        def body(c, carry):
            acc[pl.ds(pl.multiple_of(first + c * CHUNK, CHUNK), CHUNK), :] = jnp.zeros((CHUNK, acc.shape[1]), F32)
            return carry
        lax.fori_loop(0, count // CHUNK, body, 0)

    @pl.when(host)
    def _():
        half_copy(0).start()

    def first_tile(j, carry):
        load_1 = pltpu.make_async_copy(w1.at[:, tile_rows(j)], acc.at[pl.ds(0, acc.shape[1]), pl.ds(0, TILE)], l_own.at[0])
        load_2 = pltpu.make_async_copy(w2.at[tile_rows(j)], own.at[1], l_own.at[1])
        load_1.start()
        load_2.start()
        load_1.wait()
        for c in range(TILE // 128):
            turned = acc[0:acc.shape[1], c * 128:(c + 1) * 128].T
            own[0, c * 128:(c + 1) * 128, :] = turned
            ob[0, c * 128:(c + 1) * 128, :] = turned.astype(BF)
        keep = pltpu.make_async_copy(own.at[0], o1.at[tile_rows(j)], l_out.at[0])
        keep.start()
        load_2.wait()

        def cast(c, carry):
            part = pl.ds(pl.multiple_of(c * CHUNK, CHUNK), CHUNK)
            ob[1, part, :] = own[1, part, :].astype(BF)
            return carry
        lax.fori_loop(0, TILE // CHUNK, cast, 0)
        copy = pltpu.make_async_copy(ob, wb.at[0, :, tile_rows(j)], l_out.at[2])
        copy.start()
        copy.wait()
        send_tile(0, j, wb.at[0])
        keep.wait()
        return carry
    lax.fori_loop(0, nt, first_tile, 0)

    @pl.when(host)
    def _():
        def body(t, carry):
            half_copy(t).start()
            return carry
        lax.fori_loop(1, steps, body, 0)

    blocks = steps * nb

    def pre_stage(n, slot):
        stage(inp.at[n // nb, block(lax.rem(n, nb))], slot).start()

    def pre_keep(n, slot):
        return pltpu.make_async_copy(ob.at[slot], rn.at[n // nb, block(lax.rem(n, nb))], l_out.at[slot])

    pre_stage(jnp.int32(0), 0)

    def pre_norm(n, carry):
        slot = lax.rem(n, 2)

        @pl.when(n + 1 < blocks)
        def _():
            pre_stage(n + 1, 1 - slot)
        stage_wait(slot)

        @pl.when(n > 1)
        def _():
            pre_keep(n - 2, slot).wait()
        norm_rows(st.at[slot], ob.at[slot], 0)
        pre_keep(n, slot).start()
        return carry
    lax.fori_loop(0, blocks, pre_norm, 0)
    for n in (blocks - 2, blocks - 1):
        pre_keep(jnp.int32(n), n % 2).wait()

    def step(t, carry):
        @pl.when(guest)
        def _():
            half_copy(t).wait_recv()
        stage_fwd_rows(t, 0, 0)
        for m in range(hb_n):
            if m + 1 < hb_n:
                stage_fwd_rows(t, m + 1, (m + 1) % 2)
            stage_wait(m % 2)
            norm_rows(st.at[m % 2], gb, m * ROWS)
        zero(0, half_rows)

        def start_tile(i, slot):
            j = lax.rem(i, nt)

            @pl.when(jnp.logical_and(i < nt, host))
            def _():
                own_tile(t, j, slot)

            @pl.when(jnp.logical_and(i < nt, guest))
            def _():
                tile_copy(MATE, t, j, wb.at[0]).wait_recv()
                pltpu.make_async_copy(gm.at[t, :, tile_rows(j)], wall.at[slot], l_wt.at[slot]).start()

            @pl.when(i >= nt)
            def _():
                tile_copy(DEEP, t, j, wb.at[0]).wait_recv()
                pltpu.make_async_copy(zr.at[t, :, tile_rows(j)], wall.at[slot], l_wt.at[slot]).start()

            @pl.when(jnp.logical_and(i >= nt, host))
            def _():
                forward_copy(t, j).start()

        start_tile(jnp.int32(0), 0)

        def fwd_block(m, slot):
            x = dot_nt(gb[block(m), :], wall[slot, 0]) * up_scale
            cdf = 0.5 + 0.5 * jnp.tanh(x * (GELU_C + (GELU_C * GELU_A) * (x * x)))
            a = (x * cdf).astype(BF)
            acc[block(m), :] += dot_nn(a, wall[slot, 1])

        def fwd_tile(i, carry):
            slot = lax.rem(i, 2)
            wait_tile(slot)

            def body(m, carry):
                fwd_block(m, slot)

                @pl.when(m == hb_n - 2)
                def _():
                    start_tile(i + 1, 1 - slot)
                return carry
            lax.fori_loop(0, hb_n, body, 0)
            return carry
        lax.fori_loop(0, 2 * nt - 1, fwd_tile, 0)

        last = (2 * nt - 1) % 2
        stage_fwd_rows(t, jnp.int32(0), 0)
        wait_tile(last)

        def last_block(m, carry):
            slot = lax.rem(m, 2)

            @pl.when(m + 1 < hb_n)
            def _():
                stage_fwd_rows(t, m + 1, 1 - slot)
            fwd_block(m, last)
            stage_wait(slot)

            def add_rows(c, carry):
                rows = pl.ds(pl.multiple_of(c * CHUNK, CHUNK), CHUNK)
                branch = acc[pl.ds(pl.multiple_of(m * ROWS + c * CHUNK, CHUNK), CHUNK), :] * down_scale
                ob[slot, rows, :] = (st[slot, rows, :].astype(F32) + branch).astype(BF)
                return carry
            lax.fori_loop(0, ROWS // CHUNK, add_rows, 0)

            @pl.when(host)
            def _():
                out = pltpu.make_async_copy(ob.at[slot], hb.at[t, rows_of(core, m)], l_out.at[2])
                out.start()
                out.wait()
                h_host_copy(t, m).start()

            @pl.when(guest)
            def _():
                out = pltpu.make_async_copy(ob.at[slot], hs.at[t, block(m)], l_out.at[2])
                out.start()
                out.wait()
                h_guest_copy(0, t, m).start()
                h_guest_copy(1, t, m).start()
            return carry
        lax.fori_loop(0, hb_n, last_block, 0)

        def load_all(j, carry):
            own_tile(t, j, j)
            return carry
        lax.fori_loop(0, nt, load_all, 0)

        def piece(i):
            return rows_of(lax.rem(core + i, 2), i // 2)

        def load_target(i):
            slot = lax.rem(i, 2)
            return pltpu.make_async_copy(tgt.at[t, piece(i)], ob.at[slot], l_tg.at[slot])

        def load_input(i):
            slot = lax.rem(i, 2)
            return pltpu.make_async_copy(rn.at[t, piece(i)], rb.at[slot], l_rb.at[slot])

        def load_h(i):
            slot = lax.rem(i, 2)
            return pltpu.make_async_copy(hb.at[t, piece(i)], st.at[slot], l_st.at[slot])

        def await_h(i):
            half = lax.rem(core + i, 2)

            @pl.when(jnp.logical_or(guest, half != core))
            def _():
                h_wait(t, half, i // 2)
            load_h(i).start()

        def load_mix(j):
            @pl.when(host)
            def _():
                tile_copy(MATE, t, j, wb.at[0]).wait_recv()
            tile_copy(FAR, t, j, wb.at[0]).wait_recv()
            tile_copy(SIDE, t, j, wb.at[0]).wait_recv()
            for kind in (MATE, FAR, SIDE):
                for w in range(2):
                    pltpu.make_async_copy(bufs[kind].at[t, w, tile_rows(j)], gb.at[pl.ds((2 * kind + w) * TILE, TILE)],
                                          l_g.at[2 * kind + w]).start()
            pltpu.make_async_copy(o1.at[tile_rows(j)], own.at[0], l_own.at[0]).start()

            @pl.when(t == 0)
            def _():
                pltpu.make_async_copy(w2.at[tile_rows(j)], own.at[1], l_own.at[1]).start()

            @pl.when(t > 0)
            def _():
                pltpu.make_async_copy(o2.at[tile_rows(j)], own.at[1], l_own.at[1]).start()

        def wait_mix():
            for kind in (MATE, FAR, SIDE):
                for w in range(2):
                    pltpu.make_async_copy(bufs[kind].at[t, w, tile_rows(0)], gb.at[pl.ds((2 * kind + w) * TILE, TILE)],
                                          l_g.at[2 * kind + w]).wait()
            for w in range(2):
                pltpu.make_async_copy(w2.at[tile_rows(0)], own.at[w], l_own.at[w]).wait()

        def grad_rows(j, w):
            return pl.ds(pl.multiple_of((2 * j + w) * TILE, TILE), TILE)

        outs = (o1, o2)

        def keep(j, w):
            return pltpu.make_async_copy(acc.at[grad_rows(j, w)], outs[w].at[tile_rows(j)], l_of.at[j, w])

        def send_new(j):
            @pl.when(t < steps - 1)
            def _():
                pltpu.make_async_copy(ob, wb.at[t + 1, :, tile_rows(j)], l_out.at[2]).wait()
                send_tile(t + 1, j, wb.at[t + 1])

        def update_tile(j):
            wait_mix()
            for w in range(2):
                def update(c, carry):
                    part = pl.ds(pl.multiple_of(c * CHUNK, CHUNK), CHUNK)
                    at = pl.ds(pl.multiple_of((2 * j + w) * TILE + c * CHUNK, CHUNK), CHUNK)

                    def mixed(kind):
                        return gb[pl.ds(pl.multiple_of((2 * kind + w) * TILE + c * CHUNK, CHUNK), CHUNK), :].astype(F32)
                    total = own[w, part, :] + mixed(MATE) + mixed(FAR) + 2.0 * mixed(SIDE)
                    new = total * 0.2 - LEARN_RATE * acc[at, :]
                    acc[at, :] = new
                    ob[w, part, :] = new.astype(BF)
                    return carry
                lax.fori_loop(0, TILE // CHUNK, update, 0, unroll=2)
                keep(j, w).start()

            @pl.when(t < steps - 1)
            def _():
                pltpu.make_async_copy(ob, wb.at[t + 1, :, tile_rows(j)], l_out.at[2]).start()

        load_target(jnp.int32(0)).start()
        load_input(jnp.int32(0)).start()
        zero(0, 2 * nt * TILE)
        await_h(jnp.int32(0))

        def arrive(j, carry):
            wait_tile(j)
            return carry
        lax.fori_loop(0, nt, arrive, 0)

        def bwd_block(i, carry):
            slot = lax.rem(i, 2)
            final = i == nb - 1

            @pl.when(i + 1 < nb)
            def _():
                load_target(i + 1).start()
                load_input(i + 1).start()

            @pl.when(i == nb - 2)
            def _():
                load_mix(jnp.int32(0))
            load_input(i).wait()
            load_target(i).wait()
            load_h(i).wait()

            def scale(c, carry):
                part = pl.ds(pl.multiple_of(c * CHUNK, CHUNK), CHUNK)
                diff = st[slot, part, :].astype(F32) - ob[slot, part, :].astype(F32)
                st[slot, part, :] = (((2.0 / num_rows) * diff) * down_scale).astype(BF)
                return carry
            lax.fori_loop(0, ROWS // CHUNK, scale, 0, unroll=4)

            def bwd_tile(j, carry):
                r_m = rb[slot]
                go_m = st[slot]
                x = dot_nt(wall[j, 0], r_m) * up_scale
                dh = dot_nt(wall[j, 1], go_m)
                x2 = x * x
                th = jnp.tanh(x * (GELU_C + (GELU_C * GELU_A) * x2))
                cdf = 0.5 + 0.5 * th
                slope = cdf + (x * (0.5 * GELU_C + (1.5 * GELU_C * GELU_A) * x2)) * (1.0 - th * th)
                a = (x * cdf).astype(BF)
                dp = ((dh * slope) * up_scale).astype(BF)
                acc[grad_rows(j, 1), :] += dot_nn(a, go_m)
                acc[grad_rows(j, 0), :] += dot_nn(dp, r_m)

                @pl.when(jnp.logical_and(j == nt - 2, i + 1 < nb))
                def _():
                    await_h(i + 1)

                @pl.when(final)
                def _():
                    @pl.when(j > 1)
                    def _():
                        send_new(j - 1)
                    update_tile(j)

                    @pl.when(j == 0)
                    def _():
                        send_new(j)

                    @pl.when(j + 1 < nt)
                    def _():
                        load_mix(j + 1)
                return carry
            lax.fori_loop(0, nt, bwd_tile, 0)
            return carry
        lax.fori_loop(0, nb, bwd_block, 0)
        send_new(jnp.int32(nt - 1))

        def kept(j, carry):
            for w in range(2):
                keep(j, w).wait()
            return carry
        lax.fori_loop(0, nt, kept, 0)
        return carry
    lax.fori_loop(0, steps, step, 0)

    def drain(t, carry):
        def body(j, carry):
            for kind in (MATE, FAR, SIDE):
                tile_copy(kind, t, j, wb.at[0]).wait_send()

            @pl.when(guest)
            def _():
                tile_copy(DEEP, t, j, wb.at[0]).wait_send()

            @pl.when(host)
            def _():
                forward_copy(t, j).wait_send()
            return carry
        lax.fori_loop(0, nt, body, 0)

        def h_body(m, carry):
            @pl.when(host)
            def _():
                h_host_copy(t, m).wait_send()

            @pl.when(guest)
            def _():
                h_guest_copy(0, t, m).wait_send()
                h_guest_copy(1, t, m).wait_send()
            return carry
        lax.fori_loop(0, hb_n, h_body, 0)

        @pl.when(host)
        def _():
            half_copy(t).wait_send()
        return carry
    lax.fori_loop(0, steps, drain, 0)


def train(inputs, targets, w1, w2):
    steps, num_rows, model = inputs.shape
    hidden = w2.shape[0]
    nt = hidden // TILE
    half_rows = num_rows // 2
    hb_n = half_rows // ROWS
    body = functools.partial(kernel, steps, num_rows, hidden, model ** -0.5, (2 * hidden) ** -0.5)
    shard = jax.ShapeDtypeStruct((steps, 2, hidden, model), BF)
    out_shape = (
        jax.ShapeDtypeStruct(w2.shape, F32), jax.ShapeDtypeStruct(w2.shape, F32),
        jax.ShapeDtypeStruct(inputs.shape, BF),
        shard,
        jax.ShapeDtypeStruct((steps, half_rows, model), BF),
        jax.ShapeDtypeStruct(inputs.shape, BF),
        shard, shard, shard, shard,
        jax.ShapeDtypeStruct((steps, half_rows, model), BF))
    any_spec = pl.BlockSpec(memory_space=pl.ANY)
    dma = pltpu.SemaphoreType.DMA
    flops = steps * 12 * num_rows * hidden * model
    return pl.pallas_call(
        body, out_shape=out_shape, in_specs=[any_spec] * 4, out_specs=[any_spec] * len(out_shape),
        scratch_shapes=[
            pltpu.VMEM((2 * hidden, model), F32), pltpu.VMEM((nt, 2, TILE, model), BF),
            pltpu.VMEM((2, TILE, model), F32), pltpu.VMEM((6 * TILE, model), BF),
            pltpu.VMEM((2, TILE, model), BF), pltpu.VMEM((2, ROWS, model), BF), pltpu.VMEM((2, ROWS, model), BF),
            dma((4, steps, nt)), dma((4, steps, nt)), dma((steps, nt)),
            dma((2, steps, hb_n)), dma((2, steps, hb_n)), dma((steps,)), dma((steps,)),
            dma((nt,)), dma((2,)), dma((6,)), dma((2,)), dma((2,)), dma((2,)), dma((3,)), dma((nt, 2)),
        ],
        compiler_params=pltpu.CompilerParams(collective_id=0, has_side_effects=True, vmem_limit_bytes=67043328),
        cost_estimate=pl.CostEstimate(flops=flops, bytes_accessed=600000000, transcendentals=0),
        name="steps",
    )(inputs, targets, w1, w2)


def solution(mesh):
    up_spec = P("x", "y", None, None, "tp")
    down_spec = P("x", "y", None, "tp", None)
    data_spec = P("x", "y")

    def device_fn(up_block, down_block, input_block, target_block):
        outs = train(input_block[0, 0], target_block[0, 0], up_block[0, 0, 0], down_block[0, 0, 0])
        return outs[0].T[None, None, None], outs[1][None, None, None], outs[2][-1][None, None]

    def run(w_up, w_down, inputs, targets):
        return jax.shard_map(device_fn, mesh=mesh, in_specs=(up_spec, down_spec, data_spec, data_spec),
                             out_specs=(up_spec, down_spec, data_spec), check_vma=False)(w_up, w_down, inputs, targets)

    return run
```

time: 1130 us -> 971 us (0.86)
  Pallas kernels: 1060 us -> 936 us
  other arithmetic: 27.1 us -> 0 us
  local copies, waits for them, and re-layouts: 47.1 us -> 33.2 us
    pallas_call x1, Pallas kernels: 1060 us -> 936 us  [train(): pl.pallas_call(body, out_shape=out_shape, in_specs=[any_spec] * 4, out_sp...]
    another operation x2 -> x0, other arithmetic: 19 us -> none  [device_fn(): wb0 = jnp.stack([w1.astype(BF), w2.astype(BF)])]
    unnamed x3 -> x2, local copies, waits for them, and re-layouts: 38.3 us -> 24.4 us
where the time goes in v2:
time: 971 us; the launch traced here: 970 us
  Pallas kernels  936 us (96%)
  local copies, waits for them, and re-layouts  33.2 us (3%)
    pallas_call x1, Pallas kernels, train(): pl.pallas_call(body, out_shape=out_shape, in_specs=[any_spec] * 4, out_sp...  936 us
    unnamed x2, local copies, waits for them, and re-layouts  24.4 us

profile of v2, /device:TPU:10, one launch (start us, length us, event | category | flops | bytes accessed | tf_op | source)
XLA Modules:
  0.0 969.6 jit_solution(11917382655379473826)
XLA Ops:
  0.6 935.8 %steps.1 = (f32[2560,1280]{1,0:T(8,128)}, f32[2560,1280]{1,0:T(8,128)}, bf16[3,4096,1280]{2,1,0:T(8,128)(2,1)}, bf16[3,2,2560,1280]{3,2,1,0:T(8,128)(2,1)}, bf16...) custom-call(bf16[3,4096,1280]{2,1,0:T(8,128)(2,1)} %bitcast.12, ...), custom_call_target="tpu_custom_call" | custom-call | flops 483183820800 | bytes 600000000 | tf_op jit(solution)/shard_map/steps/pallas_call | solution.py:530
  936.5 13.9 %copy.7 = f32[1,1,1,1280,2560]{4,3,2,1,0:T(8,128)} copy(f32[1,1,1,1280,2560]{3,4,2,1,0:T(8,128)} %bitcast.11) | data formatting | bytes 26214400
  950.4 8.7 slice_bitcast_fusion
  959.1 10.5 %copy.9 = f32[1,1,1,2560,1280]{4,3,2,1,0:T(8,128)} copy(f32[1,1,1,2560,1280]{4,3,2,1,0:T(8,128)} %bitcast.10) | data formatting | bytes 26214400
